TPU v7x, 32 devices: a whole 2x2x4 slice. The times are simulated.
32 devices in a mesh: groups: 2 (over y), fsdp: 4 (over z), expert: 4 (over x, core).
Axes of the slice: x: 2, y: 2, z: 4, core: 2. Of those that a mesh axis runs over, the one named last changes fastest.
Arguments:
- queries: bfloat16 [512, 2048], P(('groups', 'fsdp'), 'expert'), parts along dimension 0, may hold values from -14 to 14
- keys: bfloat16 [8, 2048, 512], P(('groups', 'fsdp'), None, 'expert'), parts along dimension 0, may hold values from -14 to 14
- values: bfloat16 [8, 2048, 512], P(('groups', 'fsdp'), None, 'expert'), parts along dimension 0, may hold values from -4 to 4
- out_weight: bfloat16 [2048, 4096], P('expert', 'fsdp'), may hold values from -0.5 to 0.5
- residual: bfloat16 [512, 4096], P(('groups', 'fsdp')), parts along dimension 0, may hold values from -3 to 3
- norm_gain: float32 [4096], replicated, may hold values from 0.5 to 1.5
- route_ids: int32 [512, 2], P(('groups', 'fsdp')), parts along dimension 0, may hold values from 0 to 7, as said below
- route_slots: int32 [512, 2], P(('groups', 'fsdp')), parts along dimension 0, may hold values from 0 to 23, as said below
- route_weights: int32 [512, 2], P(('groups', 'fsdp')), parts along dimension 0, may hold values from 1 to 65535, as said below
- w_gate: bfloat16 [8, 4096, 7168], P('expert', None, 'fsdp'), may hold values from -0.09375 to 0.09375
- w_up: bfloat16 [8, 4096, 7168], P('expert', None, 'fsdp'), may hold values from -0.09375 to 0.09375
- w_down: bfloat16 [8, 7168, 4096], P('expert', 'fsdp'), may hold values from -0.0625 to 0.0625
Outputs:
- layer_out: bfloat16 [512, 4096], P(('groups', 'fsdp'), 'expert'), parts along dimension 0
There are 2 independent parts, one for each index of `groups`. A program takes and returns all parts, laid end to end along the dimension named above; an argument that names none is the same for every part. Nothing has to cross between parts.
Inputs may be any that keep to these rules, and one draw needn't show every extreme that they name: `route_ids`: each row names two different experts. Among the rows of one block, no expert is named more than 24 times and no group of experts 2 g and 2 g + 1 more than 36 times; one expert, the same for all blocks, is named exactly 24 times in every block and its group exactly 36 times; every expert is named in every block. `route_slots`: within one block, the routes to one expert hold the slots 0 to their count - 1, each once. `route_weights`: the two entries of a row sum to 65536.
All inputs are finite; a program needn't handle non-finite values.
Results may differ from a plain program's by a relative error of at most 0.02.
Values may be sent and summed in bfloat16 or wider, within the bound.
No kernel may reach another device: no remote copies, remote signals or barrier semaphores. Data moves between devices by JAX's collectives and lax.ppermute only.
A program may use at most 192 MiB of HBM per device.

v0:
```python
import jax
import jax.numpy as jnp
from jax import lax
from jax.sharding import PartitionSpec as P

HEAD_DIM = 128
GCAP = 36
eps = 1e-05


def attend(queries, keys, values):
    block = queries.shape[0]
    context = keys.shape[1]
    kv_dev = keys.shape[2] // HEAD_DIM
    heads_dev = queries.shape[1] // HEAD_DIM
    group = heads_dev // kv_dev
    query_heads = queries.reshape(block, kv_dev, group, HEAD_DIM)
    key_heads = keys[0].reshape(context, kv_dev, HEAD_DIM)
    value_heads = values[0].reshape(context, kv_dev, HEAD_DIM)
    scores = jnp.einsum(
        "qcgd,kcd->cgqk", query_heads, key_heads, preferred_element_type=jnp.float32
    ) * HEAD_DIM ** (-0.5)
    key_pos = jnp.arange(context)
    query_pos = context - block + jnp.arange(block)
    allowed = key_pos[None, :] <= query_pos[:, None]
    masked = jnp.where(allowed, scores, -1e30)
    highest = jnp.max(masked, axis=-1, keepdims=True)
    weights = jnp.where(allowed, jnp.exp(masked - highest), 0.0)
    probs = (weights / jnp.sum(weights, axis=-1, keepdims=True)).astype(jnp.bfloat16)
    heads_out = jnp.einsum("cgqk,kcd->qcgd", probs, value_heads, preferred_element_type=jnp.float32)
    return heads_out.astype(jnp.bfloat16).reshape(block, heads_dev * HEAD_DIM)


def per_device(
    queries,
    keys,
    values,
    out_weight,
    residual,
    norm_gain,
    route_ids,
    route_slots,
    route_weights,
    w_gate,
    w_up,
    w_down,
):
    heads_out = attend(queries, keys, values)
    partial_attn = jnp.dot(
        heads_out,
        lax.all_gather(out_weight, "fsdp", axis=1, tiled=True),
        preferred_element_type=jnp.float32,
    )
    attn = lax.psum(partial_attn.astype(jnp.bfloat16), "expert").astype(jnp.float32)
    hstate = (residual.astype(jnp.float32) + attn).astype(jnp.bfloat16)
    state = hstate.astype(jnp.float32)
    scale = lax.rsqrt(jnp.mean(state * state, axis=-1, keepdims=True) + eps)
    normed = (state * scale * norm_gain).astype(jnp.bfloat16)
    group_index = lax.axis_index("expert")
    first_expert = 2 * group_index
    within = route_ids - first_expert
    in_group = (within >= 0) & (within < 2)
    lead_count = jnp.sum((route_ids == first_expert).astype(jnp.int32))
    target = jnp.where(in_group, route_slots + within * lead_count, -1)
    row_ids = jnp.arange(GCAP)
    one_hot = (
        (target[None, :, 0] == row_ids[:, None]) | (target[None, :, 1] == row_ids[:, None])
    ).astype(jnp.bfloat16)
    dispatch = jnp.dot(one_hot, normed, preferred_element_type=jnp.float32).astype(jnp.bfloat16)
    second = (row_ids >= lead_count).astype(jnp.bfloat16)
    rows = lax.all_gather(dispatch, "fsdp", axis=0, tiled=True)
    labels = lax.all_gather(second, "fsdp", axis=0, tiled=True)
    gate = jnp.einsum("nd,edf->enf", rows, w_gate, preferred_element_type=jnp.float32)
    upper = jnp.einsum("nd,edf->enf", rows, w_up, preferred_element_type=jnp.float32)
    labels_f = labels.astype(jnp.float32)
    keep = jnp.stack([1.0 - labels_f, labels_f], axis=0)[:, :, None]
    values_new = (jax.nn.silu(gate) * upper * keep).astype(jnp.bfloat16)
    flat_out = lax.psum_scatter(
        jnp.einsum("enf,efd->nd", values_new, w_down, preferred_element_type=jnp.float32).astype(
            jnp.bfloat16
        ),
        "fsdp",
        scatter_dimension=0,
        tiled=True,
    ).astype(jnp.float32)
    row_index = route_slots + within * lead_count
    safe_index = jnp.where(in_group, row_index, 0)
    shares = jnp.where(in_group, route_weights.astype(jnp.float32) / 65536.0, 0.0)
    picked = jnp.take(flat_out, safe_index, axis=0)
    contrib = jnp.sum(shares[:, :, None] * picked, axis=1)
    moe = lax.psum_scatter(
        contrib.astype(jnp.bfloat16), "expert", scatter_dimension=1, tiled=True
    ).astype(jnp.float32)
    width = moe.shape[1]
    own_state = lax.dynamic_slice_in_dim(hstate, group_index * width, width, 1)
    return (own_state.astype(jnp.float32) + moe).astype(jnp.bfloat16)


def solution(mesh):
    in_specs = (
        P(("groups", "fsdp"), "expert"),
        P(("groups", "fsdp"), None, "expert"),
        P(("groups", "fsdp"), None, "expert"),
        P("expert", "fsdp"),
        P(("groups", "fsdp"), None),
        P(),
        P(("groups", "fsdp"), None),
        P(("groups", "fsdp"), None),
        P(("groups", "fsdp"), None),
        P("expert", None, "fsdp"),
        P("expert", None, "fsdp"),
        P("expert", "fsdp", None),
    )
    out_specs = P(("groups", "fsdp"), "expert")
    return jax.shard_map(
        per_device, mesh=mesh, in_specs=in_specs, out_specs=out_specs, check_vma=False
    )
```

profile of v0, /device:TPU:0, one launch (start us, length us, event | category | flops | bytes accessed | tf_op | source)
XLA Modules:
  0.0 273.5 jit_solution(8926764271031604778)
XLA Ops:
  6.5 0.7 all-gather.4.cloned.1.call-update
  7.6 1.5 fusion.39
  9.6 0.7 fusion.14
  11.1 81.3 %all-gather.4.cloned.1.call-done = bf16[512,4096]{1,0:T(8,128)(2,1)} async-done(((bf16[512,1024]{1,0:T(8,128)(2,1)}), bf16[512,4096]{1,0:T(8,128)(2,1)}) %all-gather.4.cloned.1.call-update) | async-done | bytes 4194320 | tf_op jit(solution)/shard_map/all_gather | solution.py:51
  92.4 3.9 %convolution_convert_fusion = bf16[64,4096]{1,0:T(8,128)(2,1)} fusion(bf16[512,4096]{1,0:T(8,128)(2,1)} %all-gather.4.cloned.1.call-done, bf16[8,8,4,128]{3,2,1,0:T(4,128)(2,1)S(1)} %bitcast.74), kind=kOutput, calls=%fused_computation.3 | convolution fusion | flops 268697600 | bytes 4784128 | tf_op jit(solution)/shard_map/dot_general | solution.py:49
  96.4 0.7 broadcast_select_fusion
  97.0 31.3 %all-reduce.5.cloned.1.call-done = bf16[64,4096]{1,0:T(8,128)(2,1)} async-done(((bf16[64,4096]{1,0:T(8,128)(2,1)}), bf16[64,4096]{1,0:T(8,128)(2,1)}) %all-reduce.5.cloned.1.call-update) | async-done | bytes 524304 | tf_op jit(solution)/shard_map/psum | solution.py:54
  128.4 1.3 fusion.15
  129.7 1.1 fusion.2
  132.2 0.7 compare_convert_fusion
  133.1 11.8 %all-reduce = bf16[144]{0:T(256)(128)(2,1)S(1)} all-reduce(bf16[144]{0:T(256)(128)(2,1)S(1)} %dynamic-update-slice), channel_id=1, replica_groups=mesh['groups'=2,'fsdp'=4,'expert'=4] {'fsdp'}, use_global_device_ids=true, to_apply=%add | all-reduce | flops 144 | bytes 576
  144.9 0.7 compare_and_fusion
  146.7 17.0 %all-gather.6.cloned.1.call-done = bf16[4,36,4096]{2,1,0:T(8,128)(2,1)} async-done(((bf16[1,36,4096]{2,1,0:T(8,128)(2,1)}), bf16[4,36,4096]{2,1,0:T(8,128)(2,1)}) %all-gather.6.cloned.1.call-update) | async-done | bytes 1179664 | tf_op jit(solution)/shard_map/all_gather | solution.py:71
  163.6 2.2 reshape.80
  165.9 12.0 %convolution_bitcast_fusion.2 = f32[2,144,1792]{2,1,0:T(8,128)S(1)} fusion(bf16[144,4096,1]{1,0,2:T(8,128)(2,1)} %reshape.80, bf16[2,4096,1792]{2,1,0:T(8,128)(2,1)} %param.21), kind=kOutput, calls=%fused_computation.7 | convolution fusion | flops 4227858432 | bytes 32604160 | tf_op jit(solution)/shard_map/nd,edf->enf/dot_general | solution.py:73
  177.9 22.2 %fusion.1 = bf16[144,4096]{1,0:T(8,128)(2,1)} fusion(bf16[2,1792,4096]{2,1,0:T(8,128)(2,1)} %param.23, bf16[144,4096,1]{1,0,2:T(8,128)(2,1)} %reshape.80, bf16[2,4096,1792]{2,1,0:T(8,128)(2,1)} %param.22, f32[2,144,1792]{2,1,0:T(8,128)S(1)} %convolution_bitcast_fusion.2, f32[2,144]{1,0:T(2,128)S(1)} %pad_maximum_fusion), kind=kOutput, calls=%fused_computation.2 | convolution fusion | flops 8459919360 | bytes 63145088 | tf_op jit(solution)/shard_map/enf,efd->nd/dot_general | solution.py:79
  200.1 29.1 %fusion = bf16[40,4096]{1,0:T(8,128)(2,1)S(1)} fusion(bf16[144,4096]{1,0:T(8,128)(2,1)} %fusion.1), kind=kCustom, calls=%all-reduce-scatter | all-reduce-scatter fusion | flops 655361 | bytes 1507840
  229.2 1.8 collective-permute-start
  231.0 2.3 collective-permute-done
  233.8 1.3 gather_fusion
  235.2 2.3 reshape.62
  237.4 6.0 %multiply_reduce_fusion = bf16[64,4096]{1,0:T(8,128)(2,1)} fusion(f32[64,2,4096]{2,1,0:T(2,128)} %reshape.62, pred[64,2]{1,0:T(8,128)(4,1)S(1)} %copy.25, f32[64,2]{1,0:T(8,128)S(1)} %copy.24), kind=kLoop, calls=%fused_computation.14 | loop fusion | flops 1310720 | bytes 2622080 | tf_op jit(solution)/shard_map/reduce_sum | solution.py:90
  243.5 21.9 %reduce-scatter.4.cloned.1.call-done = bf16[64,1024]{1,0:T(8,128)(2,1)} async-done(((bf16[64,4096]{1,0:T(8,128)(2,1)}), bf16[64,1024]{1,0:T(8,128)(2,1)}) %reduce-scatter.4.cloned.1.call-update) | async-done | bytes 131088 | tf_op jit(solution)/shard_map/reduce_scatter | solution.py:91
  265.4 1.7 add_convert_fusion.1
  (49 shorter events, 3.6 us)
Async XLA Ops:
  6.5 1.0 copy-start
  6.5 85.9 %all-gather.4.cloned.1.call-start = ((), (), s32[]{:S(2)}) async-start(), calls=%async_computation.1 | async-start | bytes 5242880 | tf_op jit(solution)/shard_map/all_gather | solution.py:51
  7.3 121.1 %all-reduce.5.cloned.1.call-start = ((), (), s32[]{:S(2)}) async-start(), calls=%async_computation.2 | async-start | bytes 1048576 | tf_op jit(solution)/shard_map/psum | solution.py:54
  7.6 2.0 copy-start.8
  9.6 0.8 copy-start.4
  9.6 1.5 copy-start.7
  92.4 4.0 %copy-start.5 = (s32[64,2]{0,1:T(2,128)S(1)}, s32[64,2]{0,1:T(2,128)}, u32[]{:S(2)}) copy-start(s32[64,2]{0,1:T(2,128)} %param.19) | copy-start | bytes 1540
  92.4 36.0 %copy-start.3 = (bf16[64,4096]{1,0:T(8,128)(2,1)S(1)}, bf16[64,4096]{1,0:T(8,128)(2,1)}, u32[]{:S(2)}) copy-start(bf16[64,4096]{1,0:T(8,128)(2,1)} %param.16) | copy-start | bytes 1572868
  96.3 33.4 %copy-start.9 = (f32[4096]{0:T(1024)S(1)}, f32[4096]{0:T(1024)}, u32[]{:S(2)}) copy-start(f32[4096]{0:T(1024)} %param.17) | copy-start | bytes 49156
  96.3 34.6 %copy-start.6 = (u32[32]{0:T(128)S(1)}, u32[32]{0:T(128)}, u32[]{:S(2)}) copy-start(u32[32]{0:T(128)} %constant.60) | copy-start | bytes 388
  96.3 67.3 %all-gather.6.cloned.1.call-start = ((), (), s32[]{:S(2)}) async-start(), calls=%async_computation.4 | async-start | bytes 1638400 | tf_op jit(solution)/shard_map/all_gather | solution.py:71
  129.7 48.2 %copy-start.2 = (bf16[64,4096]{1,0:T(8,128)(2,1)}, bf16[64,4096]{1,0:T(8,128)(2,1)S(1)}, u32[]{:S(2)}) copy-start(bf16[64,4096]{1,0:T(8,128)(2,1)S(1)} %get-tuple-element.10) | copy-start | bytes 1572868
  130.8 134.5 %reduce-scatter.4.cloned.1.call-start = ((), (), s32[]{:S(2)}) async-start(), calls=%async_computation.3 | async-start | bytes 655360 | tf_op jit(solution)/shard_map/reduce_scatter | solution.py:91
  229.2 4.1 %collective-permute-start = (bf16[12,4096]{1,0:T(8,128)(2,1)S(1)}, bf16[12,4096]{1,0:T(8,128)(2,1)S(1)}, u32[]{:S(2)}, u32[]{:S(2)}) collective-permute-start(bf16[12,4096]{1,0:T(8,128)(2,1)S(1)} %slice.10), channel_id=1, source_target_pairs={{0,4},{4,8},{8,12},{1,5},{5,9},{9,13},{2,6},{6,10},{10,14},{3,7},{... | collective-permute-start | bytes 294920
  235.1 31.9 %copy-start.1 = (bf16[1,2048,128]{2,1,0:T(8,128)(2,1)S(1)}, bf16[1,2048,128]{2,1,0:T(8,128)(2,1)}, u32[]{:S(2)}) copy-start(bf16[1,2048,128]{2,1,0:T(8,128)(2,1)} %param.13) | copy-start | bytes 1572868
Sparse Core Ops, SparseCore 0:
  8.9 83.4 all-gather.3
  96.4 31.8 all-reduce.4
  130.9 32.6 all-gather.5
  243.6 21.6 reduce-scatter.3
where the time goes:
time: 274 us
  waiting for transfers between devices  155 us (57%)
  matrix products  41.3 us (15%)
  blocking collectives  40.8 us (15%)
  between operations  14.7 us (5%)
  other arithmetic  12.4 us (5%)
  local copies, waits for them, and re-layouts  7.87 us (3%)
    all_gather x1, waiting for transfers between devices, per_device(): lax.all_gather(out_weight, 'fsdp', axis=1, tiled=True)  81.3 us
    unnamed x2, blocking collectives  40.8 us
    psum x1, waiting for transfers between devices, per_device(): lax.psum(partial_attn.astype(jnp.bfloat16), 'expert').astype(jnp.float32)  31.3 us
    dot_general x1, matrix products, per_device(): jnp.einsum('enf,efd->nd', values_new, w_down, preferred_element_type=jnp....  22.2 us
    reduce_scatter x1, waiting for transfers between devices, per_device(): lax.psum_scatter(contrib.astype(jnp.bfloat16), 'expert', scatter_dimensio...  21.9 us
    all_gather x1, waiting for transfers between devices, per_device(): rows = lax.all_gather(dispatch, 'fsdp', axis=0, tiled=True)  17 us
    dot_general x1, matrix products, per_device(): jnp.einsum('nd,edf->enf', rows, w_gate, preferred_element_type=jnp.float32)  12 us
    reduce_sum x1, other arithmetic, per_device(): contrib = jnp.sum(shares[:, :, None] * picked, axis=1)  6.02 us
  transfers between devices with their start and end apart: 5, of which 5 were waited for; matrix products, arithmetic and copies ran while one was open for 3% of the time, Pallas kernels for 0%

commit v1 on v0

--- a/solution.py
+++ b/solution.py
@@ -1,3 +1,4 @@
+import functools
 import jax
 import jax.numpy as jnp
 from jax import lax
@@ -6,6 +7,14 @@
 HEAD_DIM = 128
 GCAP = 36
 eps = 1e-05
+
+
+def files_do(local_values, net_axis):
+    x_next = lax.all_gather(local_values, net_axis)
+    return jnp.sum(x_next, 0)
+
+
+_find_sides = functools.partial(files_do, net_axis="expert")
 
 
 def attend(queries, keys, values):
@@ -51,7 +60,7 @@
         lax.all_gather(out_weight, "fsdp", axis=1, tiled=True),
         preferred_element_type=jnp.float32,
     )
-    attn = lax.psum(partial_attn.astype(jnp.bfloat16), "expert").astype(jnp.float32)
+    attn = _find_sides(partial_attn.astype(jnp.bfloat16)).astype(jnp.float32)
     hstate = (residual.astype(jnp.float32) + attn).astype(jnp.bfloat16)
     state = hstate.astype(jnp.float32)
     scale = lax.rsqrt(jnp.mean(state * state, axis=-1, keepdims=True) + eps)

time: 274 us -> 265 us (0.967)
  waiting for transfers between devices: 155 us -> 144 us
    psum x1 -> x0, waiting for transfers between devices: 31.3 us -> none  [per_device(): lax.psum(partial_attn.astype(jnp.bfloat16), 'expert').astype(jnp.float32)]
    all_gather x0 -> x1, waiting for transfers between devices: none -> 19.8 us  [files_do(): x_next = lax.all_gather(local_values, net_axis)]
where the time goes in v1:
time: 265 us; the launch traced here: 264 us
  waiting for transfers between devices  144 us (54%)
  matrix products  41.3 us (16%)
  blocking collectives  40.9 us (15%)
  between operations  14.7 us (6%)
  other arithmetic  13.3 us (5%)
  local copies, waits for them, and re-layouts  8.66 us (3%)
    all_gather x1, waiting for transfers between devices, per_device(): lax.all_gather(out_weight, 'fsdp', axis=1, tiled=True)  82 us
    unnamed x2, blocking collectives  40.9 us
    dot_general x1, matrix products, per_device(): jnp.einsum('enf,efd->nd', values_new, w_down, preferred_element_type=jnp....  22.2 us
    reduce_scatter x1, waiting for transfers between devices, per_device(): lax.psum_scatter(contrib.astype(jnp.bfloat16), 'expert', scatter_dimensio...  21.9 us
    all_gather x1, waiting for transfers between devices, files_do(): x_next = lax.all_gather(local_values, net_axis)  19.8 us
    all_gather x1, waiting for transfers between devices, per_device(): rows = lax.all_gather(dispatch, 'fsdp', axis=0, tiled=True)  16.9 us
    dot_general x1, matrix products, per_device(): jnp.einsum('nd,edf->enf', rows, w_gate, preferred_element_type=jnp.float32)  12 us
    reduce_sum x1, other arithmetic, per_device(): contrib = jnp.sum(shares[:, :, None] * picked, axis=1)  6.02 us
  transfers between devices with their start and end apart: 5, of which 5 were waited for; matrix products, arithmetic and copies ran while one was open for 3% of the time, Pallas kernels for 0%

profile of v1, /device:TPU:0, one launch (start us, length us, event | category | flops | bytes accessed | tf_op | source)
XLA Modules:
  0.0 264.3 jit_solution(15628697844452212698)
XLA Ops:
  6.5 0.7 all-gather.6.cloned.1.call-update
  7.6 1.5 fusion.39
  9.6 0.7 fusion.14
  10.4 82.0 %all-gather.6.cloned.1.call-done = bf16[512,4096]{1,0:T(8,128)(2,1)} async-done(((bf16[512,1024]{1,0:T(8,128)(2,1)}), bf16[512,4096]{1,0:T(8,128)(2,1)}) %all-gather.6.cloned.1.call-update) | async-done | bytes 4194320 | tf_op jit(solution)/shard_map/all_gather | solution.py:60
  92.4 3.9 %convolution_convert_fusion = bf16[64,4096]{1,0:T(8,128)(2,1)} fusion(bf16[512,4096]{1,0:T(8,128)(2,1)} %all-gather.6.cloned.1.call-done, bf16[8,8,4,128]{3,2,1,0:T(4,128)(2,1)S(1)} %bitcast.76), kind=kOutput, calls=%fused_computation.3 | convolution fusion | flops 268697600 | bytes 4784128 | tf_op jit(solution)/shard_map/dot_general | solution.py:58
  97.0 0.7 broadcast_select_fusion
  97.7 19.8 %all-gather.8.cloned.1.call-done = bf16[256,4096]{1,0:T(8,128)(2,1)} async-done(((bf16[64,4096]{1,0:T(8,128)(2,1)}), bf16[256,4096]{1,0:T(8,128)(2,1)}) %all-gather.8.cloned.1.call-update) | async-done | bytes 2097168 | tf_op jit(solution)/shard_map/all_gather | solution.py:13
  117.5 2.0 reduce_sum.49
  119.8 0.8 copy-done.2
  120.6 1.1 fusion.2
  124.0 11.8 %all-reduce = bf16[144]{0:T(256)(128)(2,1)S(1)} all-reduce(bf16[144]{0:T(256)(128)(2,1)S(1)} %dynamic-update-slice), channel_id=1, replica_groups=mesh['groups'=2,'fsdp'=4,'expert'=4] {'fsdp'}, use_global_device_ids=true, to_apply=%add | all-reduce | flops 144 | bytes 576
  135.8 0.7 compare_and_fusion
  137.6 16.9 %all-gather.10.cloned.1.call-done = bf16[4,36,4096]{2,1,0:T(8,128)(2,1)} async-done(((bf16[1,36,4096]{2,1,0:T(8,128)(2,1)}), bf16[4,36,4096]{2,1,0:T(8,128)(2,1)}) %all-gather.10.cloned.1.call-update) | async-done | bytes 1179664 | tf_op jit(solution)/shard_map/all_gather | solution.py:80
  154.5 2.2 reshape.81
  156.8 12.0 %convolution_bitcast_fusion.2 = f32[2,144,1792]{2,1,0:T(8,128)S(1)} fusion(bf16[144,4096,1]{1,0,2:T(8,128)(2,1)} %reshape.81, bf16[2,4096,1792]{2,1,0:T(8,128)(2,1)} %param.21), kind=kOutput, calls=%fused_computation.7 | convolution fusion | flops 4227858432 | bytes 32604160 | tf_op jit(solution)/shard_map/nd,edf->enf/dot_general | solution.py:82
  168.8 22.2 %fusion.1 = bf16[144,4096]{1,0:T(8,128)(2,1)} fusion(bf16[2,1792,4096]{2,1,0:T(8,128)(2,1)} %param.23, bf16[144,4096,1]{1,0,2:T(8,128)(2,1)} %reshape.81, bf16[2,4096,1792]{2,1,0:T(8,128)(2,1)} %param.22, f32[2,144,1792]{2,1,0:T(8,128)S(1)} %convolution_bitcast_fusion.2, f32[2,144]{1,0:T(2,128)S(1)} %pad_maximum_fusion), kind=kOutput, calls=%fused_computation.2 | convolution fusion | flops 8459919360 | bytes 63145088 | tf_op jit(solution)/shard_map/enf,efd->nd/dot_general | solution.py:88
  190.9 29.1 %fusion = bf16[40,4096]{1,0:T(8,128)(2,1)S(1)} fusion(bf16[144,4096]{1,0:T(8,128)(2,1)} %fusion.1), kind=kCustom, calls=%all-reduce-scatter | all-reduce-scatter fusion | flops 655361 | bytes 1507840
  220.1 1.7 collective-permute-start
  221.8 2.3 collective-permute-done
  224.6 1.3 gather_fusion
  225.9 2.3 reshape.62
  228.2 6.0 %multiply_reduce_fusion = bf16[64,4096]{1,0:T(8,128)(2,1)} fusion(f32[64,2,4096]{2,1,0:T(2,128)} %reshape.62, pred[64,2]{1,0:T(8,128)(4,1)S(1)} %copy.25, f32[64,2]{1,0:T(8,128)S(1)} %copy.24), kind=kLoop, calls=%fused_computation.14 | loop fusion | flops 1310720 | bytes 2622080 | tf_op jit(solution)/shard_map/reduce_sum | solution.py:99
  234.3 21.9 %reduce-scatter.4.cloned.1.call-done = bf16[64,1024]{1,0:T(8,128)(2,1)} async-done(((bf16[64,4096]{1,0:T(8,128)(2,1)}), bf16[64,1024]{1,0:T(8,128)(2,1)}) %reduce-scatter.4.cloned.1.call-update) | async-done | bytes 131088 | tf_op jit(solution)/shard_map/reduce_scatter | solution.py:100
  256.1 1.7 add_convert_fusion.1
  (50 shorter events, 4.6 us)
Async XLA Ops:
  6.5 1.0 copy-start
  6.5 85.9 %all-gather.6.cloned.1.call-start = ((), (), s32[]{:S(2)}) async-start(), calls=%async_computation.1 | async-start | bytes 5242880 | tf_op jit(solution)/shard_map/all_gather | solution.py:60
  7.3 110.2 %all-gather.8.cloned.1.call-start = ((), (), s32[]{:S(2)}) async-start(), calls=%async_computation.3 | async-start | bytes 2621440 | tf_op jit(solution)/shard_map/all_gather | solution.py:13
  7.6 2.0 copy-start.8
  92.4 4.0 %copy-start.4 = (s32[64,2]{0,1:T(2,128)S(1)}, s32[64,2]{0,1:T(2,128)}, u32[]{:S(2)}) copy-start(s32[64,2]{0,1:T(2,128)} %param.18) | copy-start | bytes 1540
  92.4 4.6 %copy-start.7 = (s32[64,2]{0,1:T(2,128)S(1)}, s32[64,2]{0,1:T(2,128)}, u32[]{:S(2)}) copy-start(s32[64,2]{0,1:T(2,128)} %param.20) | copy-start | bytes 1540
  92.4 4.6 %copy-start.5 = (s32[64,2]{0,1:T(2,128)S(1)}, s32[64,2]{0,1:T(2,128)}, u32[]{:S(2)}) copy-start(s32[64,2]{0,1:T(2,128)} %param.19) | copy-start | bytes 1540
  96.3 23.2 %copy-start.3 = (bf16[64,4096]{1,0:T(8,128)(2,1)S(1)}, bf16[64,4096]{1,0:T(8,128)(2,1)}, u32[]{:S(2)}) copy-start(bf16[64,4096]{1,0:T(8,128)(2,1)} %param.16) | copy-start | bytes 1572868
  96.3 58.2 %all-gather.10.cloned.1.call-start = ((), (), s32[]{:S(2)}) async-start(), calls=%async_computation.4 | async-start | bytes 1638400 | tf_op jit(solution)/shard_map/all_gather | solution.py:80
  117.5 3.1 %copy-start.9 = (f32[4096]{0:T(1024)S(1)}, f32[4096]{0:T(1024)}, u32[]{:S(2)}) copy-start(f32[4096]{0:T(1024)} %param.17) | copy-start | bytes 49156
  119.5 2.3 copy-start.6
  119.8 0.8 copy-start.2
  121.7 134.4 %reduce-scatter.4.cloned.1.call-start = ((), (), s32[]{:S(2)}) async-start(), calls=%async_computation.2 | async-start | bytes 655360 | tf_op jit(solution)/shard_map/reduce_scatter | solution.py:100
  220.1 4.0 %collective-permute-start = (bf16[12,4096]{1,0:T(8,128)(2,1)S(1)}, bf16[12,4096]{1,0:T(8,128)(2,1)S(1)}, u32[]{:S(2)}, u32[]{:S(2)}) collective-permute-start(bf16[12,4096]{1,0:T(8,128)(2,1)S(1)} %slice.10), channel_id=1, source_target_pairs={{0,4},{4,8},{8,12},{1,5},{5,9},{9,13},{2,6},{6,10},{10,14},{3,7},{... | collective-permute-start | bytes 294920
  225.9 31.9 %copy-start.1 = (bf16[1,2048,128]{2,1,0:T(8,128)(2,1)S(1)}, bf16[1,2048,128]{2,1,0:T(8,128)(2,1)}, u32[]{:S(2)}) copy-start(bf16[1,2048,128]{2,1,0:T(8,128)(2,1)} %param.13) | copy-start | bytes 1572868
Sparse Core Ops, SparseCore 0:
  8.9 83.4 all-gather.5
  96.4 21.0 all-gather.7
  121.8 32.6 all-gather.9
  234.4 21.6 reduce-scatter.3
